TPU v7x, 32 devices: a whole 2x2x4 slice. The times are simulated.
32 devices in a mesh: col: 8 (over z, y), row: 4 (over x, core).
Axes of the slice: x: 2, y: 2, z: 4, core: 2. Of those that a mesh axis runs over, the one named last changes fastest.
Arguments:
- right_side: float32 [8192, 256], P(('row', 'col')), may hold values from -6 to 6
- prior_solution: bfloat16 [16384, 256], P('col'), may hold values from -6 to 6
- factor_codes: bfloat16 [8192, 16384], P('row', 'col'), may hold values from -0.046875 to 0.046875
- block_scale: float32 [4, 64], P('row', 'col'), may hold values from 0.3 to 3
- diag_inverse: bfloat16 [4, 2048, 2048], P('row', 'col'), may hold values from -0.125 to 0.125
- inner_factor: bfloat16 [4, 4, 2048, 2048], P('row', None, 'col'), may hold values from -0.125 to 0.125
Outputs:
- solved: float32 [8192, 256], P(('row', 'col'))
All inputs are finite; a program needn't handle non-finite values.
Results may differ from a plain program's by a relative error of at most 0.0095.
Values may be sent and summed in bfloat16 or wider, within the bound.
No kernel may reach another device: no remote copies, remote signals or barrier semaphores. Data moves between devices by JAX's collectives and lax.ppermute only.
A program may use at most 64 MiB of HBM per device.

v0:
```python
import jax
import jax.numpy as jnp
from jax import lax
from jax.sharding import PartitionSpec as P


def from_root(value, axis, source):
    kept = jnp.where(lax.axis_index(axis) == source, value, 0).astype(value.dtype)
    return lax.psum(kept, axis)


def local(right_side, prior_solution, factor_codes, block_scale, diag_inverse, inner_factor):
    rows_each = right_side.shape[0]
    panel_rows = factor_codes.shape[0]
    blocks_here = block_scale.shape[1]
    block_cols = factor_codes.shape[1] // blocks_here
    columns_out = right_side.shape[1]
    summed = jnp.zeros((panel_rows, columns_out), jnp.float32)
    for column_block in range(blocks_here):
        coded = lax.dynamic_slice(
            factor_codes, (0, column_block * block_cols), (panel_rows, block_cols)
        )
        earlier = prior_solution[column_block * block_cols : (column_block + 1) * block_cols]
        summed = summed + block_scale[0, column_block] * jnp.dot(
            coded, earlier, preferred_element_type=jnp.float32
        )
    prior_rows = lax.psum_scatter(summed, "col", scatter_dimension=0, tiled=True)
    rhs = right_side - prior_rows
    row_place = lax.axis_index("row")
    solved = jnp.zeros((rows_each, columns_out), jnp.float32)
    inverse_rows = diag_inverse[0]
    panel_count = lax.axis_size("row")
    for section in range(panel_count):
        rounded = rhs.astype(jnp.bfloat16)
        current = jnp.dot(
            inverse_rows,
            lax.all_gather(rounded, "col", axis=0, tiled=True),
            preferred_element_type=jnp.float32,
        )
        solved = jnp.where(row_place == section, current, solved)
        if section + 1 < panel_count:
            sending = current.astype(jnp.bfloat16)
            coupling = inner_factor[0, section]
            whole_panel = lax.all_gather(sending, "col", axis=0, tiled=True)
            copied = from_root(whole_panel, "row", section)
            update = jnp.dot(coupling, copied, preferred_element_type=jnp.float32)
            rhs = rhs - jnp.where(row_place > section, update, 0.0)
    return solved


def solution(mesh):
    return jax.shard_map(
        local,
        mesh=mesh,
        in_specs=(
            P(("row", "col"), None),
            P("col", None),
            P("row", "col"),
            P("row", "col"),
            P("row", "col", None),
            P("row", None, "col", None),
        ),
        out_specs=P(("row", "col"), None),
        check_vma=False,
    )
```

profile of v0, /device:TPU:0, one launch (start us, length us, event | category | flops | bytes accessed | tf_op | source)
XLA Modules:
  0.0 509.4 jit_solution(15707440207164434849)
XLA Ops:
  8.2 2.5 convolution_multiply_fusion.7
  10.7 2.5 fusion.6
  13.3 2.0 fusion.5
  19.6 2.4 fusion
  22.1 71.2 %reduce-scatter.2.cloned.1.call-done = f32[256,256]{1,0:T(8,128)} async-done(((f32[2048,256]{1,0:T(8,128)}), f32[256,256]{1,0:T(8,128)}) %reduce-scatter.2.cloned.1.call-update) | async-done | bytes 262160 | tf_op jit(solution)/shard_map/reduce_scatter | solution.py:27
  93.2 1.6 fusion.44
  95.0 39.7 %all-gather.8.cloned.1.call-done = bf16[2048,256]{1,0:T(8,128)(2,1)} async-done(((bf16[256,256]{1,0:T(8,128)(2,1)}), bf16[2048,256]{1,0:T(8,128)(2,1)}) %all-gather.8.cloned.1.call-update) | async-done | bytes 1048592 | tf_op jit(solution)/shard_map/all_gather | solution.py:37
  134.7 1.7 fusion.23
  137.2 38.2 %all-gather.10.cloned.1.call-done = bf16[2048,256]{0,1:T(8,128)(2,1)} async-done(((bf16[256,256]{0,1:T(8,128)(2,1)}), bf16[2048,256]{0,1:T(8,128)(2,1)}) %all-gather.10.cloned.1.call-update) | async-done | bytes 1048592 | tf_op jit(solution)/shard_map/all_gather | solution.py:44
  175.4 2.3 broadcast_select_fusion.2
  177.7 35.2 %all-reduce.4.cloned.1.call-done = bf16[2048,256]{0,1:T(8,128)(2,1)} async-done(((bf16[2048,256]{0,1:T(8,128)(2,1)}), bf16[2048,256]{0,1:T(8,128)(2,1)}) %all-reduce.4.cloned.1.call-update) | async-done | bytes 1048592 | tf_op jit(solution)/shard_map/psum | solution.py:9
  212.9 2.7 fusion.46
  215.7 40.9 %all-gather.12.cloned.1.call-done = bf16[2048,256]{1,0:T(8,128)(2,1)} async-done(((bf16[256,256]{1,0:T(8,128)(2,1)}), bf16[2048,256]{1,0:T(8,128)(2,1)}) %all-gather.12.cloned.1.call-update) | async-done | bytes 1048592 | tf_op jit(solution)/shard_map/all_gather | solution.py:37
  256.5 1.7 fusion.21
  259.0 38.2 %all-gather.14.cloned.1.call-done = bf16[2048,256]{0,1:T(8,128)(2,1)} async-done(((bf16[256,256]{0,1:T(8,128)(2,1)}), bf16[2048,256]{0,1:T(8,128)(2,1)}) %all-gather.14.cloned.1.call-update) | async-done | bytes 1048592 | tf_op jit(solution)/shard_map/all_gather | solution.py:44
  298.3 36.5 %all-reduce.6.cloned.1.call-done = bf16[2048,256]{0,1:T(8,128)(2,1)} async-done(((bf16[2048,256]{0,1:T(8,128)(2,1)}), bf16[2048,256]{0,1:T(8,128)(2,1)}) %all-reduce.6.cloned.1.call-update) | async-done | bytes 1048592 | tf_op jit(solution)/shard_map/psum | solution.py:9
  334.9 2.7 fusion.47
  337.6 40.9 %all-gather.16.cloned.1.call-done = bf16[2048,256]{1,0:T(8,128)(2,1)} async-done(((bf16[256,256]{1,0:T(8,128)(2,1)}), bf16[2048,256]{1,0:T(8,128)(2,1)}) %all-gather.16.cloned.1.call-update) | async-done | bytes 1048592 | tf_op jit(solution)/shard_map/all_gather | solution.py:37
  378.5 1.7 fusion.19
  381.0 38.2 %all-gather.18.cloned.1.call-done = bf16[2048,256]{0,1:T(8,128)(2,1)} async-done(((bf16[256,256]{0,1:T(8,128)(2,1)}), bf16[2048,256]{0,1:T(8,128)(2,1)}) %all-gather.18.cloned.1.call-update) | async-done | bytes 1048592 | tf_op jit(solution)/shard_map/all_gather | solution.py:44
  420.3 36.6 %all-reduce.8.cloned.1.call-done = bf16[2048,256]{0,1:T(8,128)(2,1)} async-done(((bf16[2048,256]{0,1:T(8,128)(2,1)}), bf16[2048,256]{0,1:T(8,128)(2,1)}) %all-reduce.8.cloned.1.call-update) | async-done | bytes 1048592 | tf_op jit(solution)/shard_map/psum | solution.py:9
  456.9 2.7 fusion.14
  460.0 40.5 %all-gather.20.cloned.1.call-done = bf16[2048,256]{1,0:T(8,128)(2,1)} async-done(((bf16[256,256]{1,0:T(8,128)(2,1)}), bf16[2048,256]{1,0:T(8,128)(2,1)}) %all-gather.20.cloned.1.call-update) | async-done | bytes 1048592 | tf_op jit(solution)/shard_map/all_gather | solution.py:37
  500.5 2.4 fusion.7
  (43 shorter events, 11.0 us)
Async XLA Ops:
  6.5 128.2 %copy-start = (bf16[1,256,2048]{2,1,0:T(8,128)(2,1)S(1)}, bf16[1,256,2048]{2,1,0:T(8,128)(2,1)}, u32[]{:S(2)}) copy-start(bf16[1,256,2048]{2,1,0:T(8,128)(2,1)} %param.10) | copy-start | bytes 3145732
  6.5 86.7 %reduce-scatter.2.cloned.1.call-start = ((), (), s32[]{:S(2)}) async-start(), calls=%async_computation.1 | async-start | bytes 2359296 | tf_op jit(solution)/shard_map/reduce_scatter | solution.py:27
  8.2 5.1 copy-start.1
  13.3 2.0 copy-start.2
  22.0 71.2 %copy-start.3 = (f32[256,256]{1,0:T(8,128)S(1)}, f32[256,256]{1,0:T(8,128)}, u32[]{:S(2)}) copy-start(f32[256,256]{1,0:T(8,128)} %param.6) | copy-start | bytes 786436
  22.0 112.7 %all-gather.8.cloned.1.call-start = ((), (), s32[]{:S(2)}) async-start(), calls=%async_computation.2 | async-start | bytes 1179648 | tf_op jit(solution)/shard_map/all_gather | solution.py:37
  94.9 80.5 %all-gather.10.cloned.1.call-start = ((), (), s32[]{:S(2)}) async-start(), calls=%async_computation.3 | async-start | bytes 1179648 | tf_op jit(solution)/shard_map/all_gather | solution.py:44
  137.1 75.8 %all-reduce.4.cloned.1.call-start = ((), (), s32[]{:S(2)}) async-start(), calls=%async_computation.4 | async-start | bytes 2097152 | tf_op jit(solution)/shard_map/psum | solution.py:9
  177.7 78.9 %all-gather.12.cloned.1.call-start = ((), (), s32[]{:S(2)}) async-start(), calls=%async_computation.5 | async-start | bytes 1179648 | tf_op jit(solution)/shard_map/all_gather | solution.py:37
  215.6 81.6 %all-gather.14.cloned.1.call-start = ((), (), s32[]{:S(2)}) async-start(), calls=%async_computation.6 | async-start | bytes 1179648 | tf_op jit(solution)/shard_map/all_gather | solution.py:44
  258.9 75.9 %all-reduce.6.cloned.1.call-start = ((), (), s32[]{:S(2)}) async-start(), calls=%async_computation.7 | async-start | bytes 2097152 | tf_op jit(solution)/shard_map/psum | solution.py:9
  298.3 80.2 %all-gather.16.cloned.1.call-start = ((), (), s32[]{:S(2)}) async-start(), calls=%async_computation.8 | async-start | bytes 1179648 | tf_op jit(solution)/shard_map/all_gather | solution.py:37
  337.6 81.6 %all-gather.18.cloned.1.call-start = ((), (), s32[]{:S(2)}) async-start(), calls=%async_computation.9 | async-start | bytes 1179648 | tf_op jit(solution)/shard_map/all_gather | solution.py:44
  380.9 76.0 %all-reduce.8.cloned.1.call-start = ((), (), s32[]{:S(2)}) async-start(), calls=%async_computation.10 | async-start | bytes 2097152 | tf_op jit(solution)/shard_map/psum | solution.py:9
  420.2 80.3 %all-gather.20.cloned.1.call-start = ((), (), s32[]{:S(2)}) async-start(), calls=%async_computation.11 | async-start | bytes 1179648 | tf_op jit(solution)/shard_map/all_gather | solution.py:37
Sparse Core Ops, SparseCore 0:
  22.2 71.0 reduce-scatter.1
  95.4 39.2 all-gather.7
  137.2 38.0 all-gather.9
  177.8 35.0 all-reduce.3
  215.8 40.7 all-gather.11
  259.1 38.0 all-gather.13
  299.6 35.2 all-reduce.5
  337.7 40.7 all-gather.15
  381.0 38.0 all-gather.17
  421.4 35.4 all-reduce.7
  459.7 40.7 all-gather.19
where the time goes:
time: 510 us; the launch traced here: 509 us
  waiting for transfers between devices  456 us (89%)
  matrix products  29.3 us (6%)
  between operations  13.4 us (3%)
  other arithmetic  8.06 us (2%)
    all_gather x4, waiting for transfers between devices, local(): lax.all_gather(rounded, 'col', axis=0, tiled=True)  162 us
    all_gather x3, waiting for transfers between devices, local(): whole_panel = lax.all_gather(sending, 'col', axis=0, tiled=True)  115 us
    psum x3, waiting for transfers between devices, from_root(): return lax.psum(kept, axis)  108 us
    reduce_scatter x1, waiting for transfers between devices, local(): lax.psum_scatter(summed, 'col', scatter_dimension=0, tiled=True)  71.2 us
    dot_general x8, matrix products, local(): jnp.dot(coded, earlier, preferred_element_type=jnp.float32)  13.7 us
  transfers between devices with their start and end apart: 11, of which 11 were waited for; matrix products, arithmetic and copies ran while one was open for 0% of the time, Pallas kernels for 0%

commit v1 on v0

--- a/solution.py
+++ b/solution.py
@@ -6,7 +6,12 @@
 
 def from_root(value, axis, source):
     kept = jnp.where(lax.axis_index(axis) == source, value, 0).astype(value.dtype)
-    return lax.psum(kept, axis)
+
+    def recover_figure(payload):
+        lower = jnp.sum(lax.all_gather(payload, axis), 0)
+        return lower
+
+    return recover_figure(kept)
 
 
 def local(right_side, prior_solution, factor_codes, block_scale, diag_inverse, inner_factor):

time: 510 us -> 547 us (1.073)
  local copies, waits for them, and re-layouts: 2.03 us -> 25.7 us
  other arithmetic: 8.06 us -> 30.2 us
  waiting for transfers between devices: 456 us -> 447 us
    psum x3 -> x0, waiting for transfers between devices: 108 us -> none  [from_root(): return lax.psum(kept, axis)]
    all_gather x0 -> x3, waiting for transfers between devices: none -> 101 us  [recover_figure(): lower = jnp.sum(lax.all_gather(payload, axis), 0)]
    all_gather x0 -> x3, local copies, waits for them, and re-layouts: none -> 23.7 us  [recover_figure(): lower = jnp.sum(lax.all_gather(payload, axis), 0)]
    reduce_sum x0 -> x3, other arithmetic: none -> 22 us  [recover_figure(): lower = jnp.sum(lax.all_gather(payload, axis), 0)]
where the time goes in v1:
time: 547 us; the launch traced here: 546 us
  waiting for transfers between devices  447 us (82%)
  other arithmetic  30.2 us (6%)
  matrix products  28.3 us (5%)
  local copies, waits for them, and re-layouts  25.7 us (5%)
  between operations  13.4 us (2%)
    all_gather x4, waiting for transfers between devices, local(): lax.all_gather(rounded, 'col', axis=0, tiled=True)  161 us
    all_gather x3, waiting for transfers between devices, local(): whole_panel = lax.all_gather(sending, 'col', axis=0, tiled=True)  115 us
    all_gather x3, waiting for transfers between devices, recover_figure(): lower = jnp.sum(lax.all_gather(payload, axis), 0)  101 us
    reduce_scatter x1, waiting for transfers between devices, local(): lax.psum_scatter(summed, 'col', scatter_dimension=0, tiled=True)  71.2 us
    all_gather x3, local copies, waits for them, and re-layouts, recover_figure(): lower = jnp.sum(lax.all_gather(payload, axis), 0)  23.7 us
    reduce_sum x3, other arithmetic, recover_figure(): lower = jnp.sum(lax.all_gather(payload, axis), 0)  22 us
    dot_general x8, matrix products, local(): jnp.dot(coded, earlier, preferred_element_type=jnp.float32)  13.7 us
  transfers between devices with their start and end apart: 11, of which 11 were waited for; matrix products, arithmetic and copies ran while one was open for 0% of the time, Pallas kernels for 0%

profile of v1, /device:TPU:0, one launch (start us, length us, event | category | flops | bytes accessed | tf_op | source)
XLA Modules:
  0.0 545.9 jit_solution(1188398663806459015)
XLA Ops:
  8.2 2.5 convolution_multiply_fusion.7
  10.7 2.5 fusion.6
  19.6 2.4 fusion
  22.1 71.2 %reduce-scatter.2.cloned.1.call-done = f32[256,256]{1,0:T(8,128)} async-done(((f32[2048,256]{1,0:T(8,128)}), f32[256,256]{1,0:T(8,128)}) %reduce-scatter.2.cloned.1.call-update) | async-done | bytes 262160 | tf_op jit(solution)/shard_map/reduce_scatter | solution.py:32
  95.0 39.7 %all-gather.14.cloned.1.call-done = bf16[2048,256]{1,0:T(8,128)(2,1)} async-done(((bf16[256,256]{1,0:T(8,128)(2,1)}), bf16[2048,256]{1,0:T(8,128)(2,1)}) %all-gather.14.cloned.1.call-update) | async-done | bytes 1048592 | tf_op jit(solution)/shard_map/all_gather | solution.py:42
  137.2 38.2 %all-gather.16.cloned.1.call-done = bf16[2048,256]{0,1:T(8,128)(2,1)} async-done(((bf16[256,256]{0,1:T(8,128)(2,1)}), bf16[2048,256]{0,1:T(8,128)(2,1)}) %all-gather.16.cloned.1.call-update) | async-done | bytes 1048592 | tf_op jit(solution)/shard_map/all_gather | solution.py:49
  177.8 32.7 %all-gather.28.cloned.1.call-done = bf16[8192,256]{0,1:T(8,128)(2,1)} async-done(((bf16[2048,256]{0,1:T(8,128)(2,1)}), bf16[8192,256]{0,1:T(8,128)(2,1)}) %all-gather.28.cloned.1.call-update) | async-done | bytes 4194320 | tf_op jit(solution)/shard_map/all_gather | solution.py:11
  210.5 7.9 %reshape = bf16[4,2048,256]{1,0,2:T(4,128)(2,1)} reshape(bf16[8192,256]{0,1:T(8,128)(2,1)} %all-gather.28.cloned.1.call-done) | data formatting | bytes 8388608 | tf_op jit(solution)/shard_map/all_gather | solution.py:11
  218.4 7.3 %reduce_sum.36 = bf16[2048,256]{0,1:T(8,128)(2,1)S(1)} reduce(bf16[4,2048,256]{1,0,2:T(4,128)(2,1)} %reshape, bf16[]{:T(256)} %constant.16.clone.1), dimensions={0}, to_apply=%region_1.2 | reduce | flops 1572864 | bytes 5242882 | tf_op jit(solution)/shard_map/reduce_sum | solution.py:11
  225.7 2.4 fusion.46
  228.1 40.4 %all-gather.18.cloned.1.call-done = bf16[2048,256]{1,0:T(8,128)(2,1)} async-done(((bf16[256,256]{1,0:T(8,128)(2,1)}), bf16[2048,256]{1,0:T(8,128)(2,1)}) %all-gather.18.cloned.1.call-update) | async-done | bytes 1048592 | tf_op jit(solution)/shard_map/all_gather | solution.py:42
  271.0 38.2 %all-gather.20.cloned.1.call-done = bf16[2048,256]{0,1:T(8,128)(2,1)} async-done(((bf16[256,256]{0,1:T(8,128)(2,1)}), bf16[2048,256]{0,1:T(8,128)(2,1)}) %all-gather.20.cloned.1.call-update) | async-done | bytes 1048592 | tf_op jit(solution)/shard_map/all_gather | solution.py:49
  310.5 33.7 %all-gather.30.cloned.1.call-done = bf16[8192,256]{0,1:T(8,128)(2,1)} async-done(((bf16[2048,256]{0,1:T(8,128)(2,1)}), bf16[8192,256]{0,1:T(8,128)(2,1)}) %all-gather.30.cloned.1.call-update) | async-done | bytes 4194320 | tf_op jit(solution)/shard_map/all_gather | solution.py:11
  344.3 7.9 %reshape.1 = bf16[4,2048,256]{1,0,2:T(4,128)(2,1)} reshape(bf16[8192,256]{0,1:T(8,128)(2,1)} %all-gather.30.cloned.1.call-done) | data formatting | bytes 8388608 | tf_op jit(solution)/shard_map/all_gather | solution.py:11
  352.2 7.3 %reduce_sum.37 = bf16[2048,256]{0,1:T(8,128)(2,1)S(1)} reduce(bf16[4,2048,256]{1,0,2:T(4,128)(2,1)} %reshape.1, bf16[]{:T(256)} %constant.16.clone.1), dimensions={0}, to_apply=%region_2.3 | reduce | flops 1572864 | bytes 5242882 | tf_op jit(solution)/shard_map/reduce_sum | solution.py:11
  359.5 2.4 fusion.47
  362.0 40.4 %all-gather.22.cloned.1.call-done = bf16[2048,256]{1,0:T(8,128)(2,1)} async-done(((bf16[256,256]{1,0:T(8,128)(2,1)}), bf16[2048,256]{1,0:T(8,128)(2,1)}) %all-gather.22.cloned.1.call-update) | async-done | bytes 1048592 | tf_op jit(solution)/shard_map/all_gather | solution.py:42
  404.8 38.2 %all-gather.24.cloned.1.call-done = bf16[2048,256]{0,1:T(8,128)(2,1)} async-done(((bf16[256,256]{0,1:T(8,128)(2,1)}), bf16[2048,256]{0,1:T(8,128)(2,1)}) %all-gather.24.cloned.1.call-update) | async-done | bytes 1048592 | tf_op jit(solution)/shard_map/all_gather | solution.py:49
  444.4 34.6 %all-gather.32.cloned.1.call-done = bf16[8192,256]{0,1:T(8,128)(2,1)} async-done(((bf16[2048,256]{0,1:T(8,128)(2,1)}), bf16[8192,256]{0,1:T(8,128)(2,1)}) %all-gather.32.cloned.1.call-update) | async-done | bytes 4194320 | tf_op jit(solution)/shard_map/all_gather | solution.py:11
  479.0 7.9 %reshape.2 = bf16[4,2048,256]{1,0,2:T(4,128)(2,1)} reshape(bf16[8192,256]{0,1:T(8,128)(2,1)} %all-gather.32.cloned.1.call-done) | data formatting | bytes 8388608 | tf_op jit(solution)/shard_map/all_gather | solution.py:11
  486.9 7.3 %reduce_sum.38 = bf16[2048,256]{0,1:T(8,128)(2,1)S(1)} reduce(bf16[4,2048,256]{1,0,2:T(4,128)(2,1)} %reshape.2, bf16[]{:T(256)} %constant.16.clone.1), dimensions={0}, to_apply=%region_3.4 | reduce | flops 1572864 | bytes 5242882 | tf_op jit(solution)/shard_map/reduce_sum | solution.py:11
  494.2 2.4 fusion.14
  497.0 40.0 %all-gather.26.cloned.1.call-done = bf16[2048,256]{1,0:T(8,128)(2,1)} async-done(((bf16[256,256]{1,0:T(8,128)(2,1)}), bf16[2048,256]{1,0:T(8,128)(2,1)}) %all-gather.26.cloned.1.call-update) | async-done | bytes 1048592 | tf_op jit(solution)/shard_map/all_gather | solution.py:42
  537.0 2.4 fusion.7
  (49 shorter events, 22.5 us)
Async XLA Ops:
  6.5 128.2 %copy-start = (bf16[1,256,2048]{2,1,0:T(8,128)(2,1)S(1)}, bf16[1,256,2048]{2,1,0:T(8,128)(2,1)}, u32[]{:S(2)}) copy-start(bf16[1,256,2048]{2,1,0:T(8,128)(2,1)} %param.10) | copy-start | bytes 3145732
  6.5 86.8 %reduce-scatter.2.cloned.1.call-start = ((), (), s32[]{:S(2)}) async-start(), calls=%async_computation.1 | async-start | bytes 2359296 | tf_op jit(solution)/shard_map/reduce_scatter | solution.py:32
  8.2 5.1 copy-start.1
  13.3 2.0 copy-start.2
  22.0 71.3 %copy-start.3 = (f32[256,256]{1,0:T(8,128)S(1)}, f32[256,256]{1,0:T(8,128)}, u32[]{:S(2)}) copy-start(f32[256,256]{1,0:T(8,128)} %param.6) | copy-start | bytes 786436
  22.0 112.7 %all-gather.14.cloned.1.call-start = ((), (), s32[]{:S(2)}) async-start(), calls=%async_computation.2 | async-start | bytes 1179648 | tf_op jit(solution)/shard_map/all_gather | solution.py:42
  95.0 80.5 %all-gather.16.cloned.1.call-start = ((), (), s32[]{:S(2)}) async-start(), calls=%async_computation.3 | async-start | bytes 1179648 | tf_op jit(solution)/shard_map/all_gather | solution.py:49
  137.1 73.3 %all-gather.28.cloned.1.call-start = ((), (), s32[]{:S(2)}) async-start(), calls=%async_computation.9 | async-start | bytes 5242880 | tf_op jit(solution)/shard_map/all_gather | solution.py:11
  177.7 90.8 %all-gather.18.cloned.1.call-start = ((), (), s32[]{:S(2)}) async-start(), calls=%async_computation.4 | async-start | bytes 1179648 | tf_op jit(solution)/shard_map/all_gather | solution.py:42
  228.1 81.1 %all-gather.20.cloned.1.call-start = ((), (), s32[]{:S(2)}) async-start(), calls=%async_computation.5 | async-start | bytes 1179648 | tf_op jit(solution)/shard_map/all_gather | solution.py:49
  270.9 73.3 %all-gather.30.cloned.1.call-start = ((), (), s32[]{:S(2)}) async-start(), calls=%async_computation.10 | async-start | bytes 5242880 | tf_op jit(solution)/shard_map/all_gather | solution.py:11
  310.3 92.0 %all-gather.22.cloned.1.call-start = ((), (), s32[]{:S(2)}) async-start(), calls=%async_computation.6 | async-start | bytes 1179648 | tf_op jit(solution)/shard_map/all_gather | solution.py:42
  361.9 81.1 %all-gather.24.cloned.1.call-start = ((), (), s32[]{:S(2)}) async-start(), calls=%async_computation.7 | async-start | bytes 1179648 | tf_op jit(solution)/shard_map/all_gather | solution.py:49
  404.7 74.2 %all-gather.32.cloned.1.call-start = ((), (), s32[]{:S(2)}) async-start(), calls=%async_computation.11 | async-start | bytes 5242880 | tf_op jit(solution)/shard_map/all_gather | solution.py:11
  444.1 92.9 %all-gather.26.cloned.1.call-start = ((), (), s32[]{:S(2)}) async-start(), calls=%async_computation.8 | async-start | bytes 1179648 | tf_op jit(solution)/shard_map/all_gather | solution.py:42
Sparse Core Ops, SparseCore 0:
  22.2 71.0 reduce-scatter.1
  95.4 39.2 all-gather.13
  137.3 38.0 all-gather.15
  177.9 32.5 all-gather.27
  228.2 40.2 all-gather.17
  271.1 38.0 all-gather.19
  310.8 33.4 all-gather.29
  362.0 40.2 all-gather.21
  404.9 38.0 all-gather.23
  444.4 34.4 all-gather.31
  496.7 40.2 all-gather.25
